TPU v7x, 32 devices: a whole 2x2x4 slice. The times are simulated.
32 devices in a mesh: expert: 8 (over z, core), hidden: 4 (over y, x).
Axes of the slice: x: 2, y: 2, z: 4, core: 2. Of those that a mesh axis runs over, the one named last changes fastest.
Arguments:
- inputs: bfloat16 [1536, 2880], P('expert', 'hidden'), may hold values from -6 to 6
- out_grad: bfloat16 [1536, 2880], P('expert', 'hidden'), may hold values from -6 to 6
- expert_ids: int32 [1536, 4], P('expert'), may hold values from 0 to 7, all different within a row; in each aligned block of 192 rows (0 to 191, 192 to 383, ...) at most 144 rows name the same one
- route_weight: float32 [1536, 4], P('expert'), may hold values from 0.1 to 1
- w_gate: bfloat16 [8, 2880, 2880], P('expert', 'hidden'), may hold values from -0.109375 to 0.109375
- w_up: bfloat16 [8, 2880, 2880], P('expert', 'hidden'), may hold values from -0.109375 to 0.109375
- w_down: bfloat16 [8, 2880, 2880], P('expert', 'hidden'), may hold values from -0.109375 to 0.109375
Outputs:
- grad_input: bfloat16 [1536, 2880], P('expert', 'hidden')
- grad_route: float32 [1536, 4], P('expert')
- grad_gate: float32 [8, 2880, 2880], P('expert', 'hidden')
- grad_up: float32 [8, 2880, 2880], P('expert', 'hidden')
- grad_down: float32 [8, 2880, 2880], P('expert', 'hidden')
Inputs may be any that keep to these rules, and one draw needn't show every extreme that they name: `expert_ids`: each token names 4 different experts. Among the 192 tokens of one index of the expert axis no expert is named more than 144 times, a bound that some block reaches.
All inputs are finite; a program needn't handle non-finite values.
Results may differ from a plain program's by a relative error of at most 0.018.
Values may be sent and summed in bfloat16 or wider, within the bound.
A program may use at most 128 MiB of HBM per device.

v0:
```python
import functools

import jax
import jax.numpy as jnp
from jax import lax
from jax.experimental import pallas as pl
from jax.experimental.pallas import tpu as pltpu
from jax.sharding import PartitionSpec as P


def slot_tables(expert_ids, experts, capacity):
    count, top = expert_ids.shape
    flat = expert_ids.reshape(-1)
    onehot = (flat[:, None] == jnp.arange(experts, dtype=jnp.int32)[None, :]).astype(jnp.int32)
    position = jnp.cumsum(onehot, axis=0) - 1
    slot = jnp.sum(onehot * position, axis=1)
    dest = flat * capacity + slot
    table = (
        jnp.zeros((experts * capacity,), jnp.int32)
        .at[dest]
        .set(jnp.arange(count * top, dtype=jnp.int32))
    )
    filled = jnp.zeros((experts * capacity,), jnp.int32).at[dest].set(1)
    return (dest, table, filled)


def pack_rows(values, table, filled, top, experts, capacity):
    picked = values[table // top] * filled.astype(values.dtype)[:, None]
    return picked.reshape(experts, capacity, values.shape[1])


def to_local(buffer, n_groups, local_count):
    rest = buffer.shape[2:]
    shaped = buffer.reshape((n_groups, local_count, buffer.shape[1]) + rest)
    return jnp.swapaxes(shaped, 0, 1).reshape((local_count, n_groups * buffer.shape[1]) + rest)


def from_local(buffer, n_groups, capacity):
    local_count = buffer.shape[0]
    rest = buffer.shape[2:]
    shaped = buffer.reshape((local_count, n_groups, capacity) + rest)
    return jnp.swapaxes(shaped, 0, 1).reshape((n_groups * local_count, capacity) + rest)


def plain_device(inputs, out_grad, expert_ids, route_weight, w_gate, w_up, w_down):
    n_groups = lax.axis_size("expert")
    local_count = w_gate.shape[0]
    experts = local_count * n_groups
    tok_count, top = expert_ids.shape
    capacity = 3 * top * tok_count // (2 * experts)
    dest, table, filled = slot_tables(expert_ids, experts, capacity)
    send_weight = (route_weight.reshape(-1)[table] * filled.astype(jnp.float32)).reshape(
        experts, capacity
    )
    send_x = pack_rows(inputs, table, filled, top, experts, capacity)
    send_dy = pack_rows(out_grad, table, filled, top, experts, capacity)
    got_x, got_dy, got_weight = (
        lax.all_to_all(send_x, "expert", split_axis=0, concat_axis=0, tiled=True),
        lax.all_to_all(send_dy, "expert", split_axis=0, concat_axis=0, tiled=True),
        lax.all_to_all(
            send_weight.astype(jnp.bfloat16), "expert", split_axis=0, concat_axis=0, tiled=True
        ).astype(send_weight.dtype),
    )
    rows_x, rows_dy = (
        lax.all_gather(got_x, "hidden", axis=2, tiled=True),
        lax.all_gather(got_dy, "hidden", axis=2, tiled=True),
    )
    xs = to_local(rows_x, n_groups, local_count)
    dys = to_local(rows_dy, n_groups, local_count)
    weights = to_local(got_weight, n_groups, local_count)
    gate = jnp.einsum("esd,efd->esf", xs, w_gate, preferred_element_type=jnp.float32)
    up = jnp.einsum("esd,efd->esf", xs, w_up, preferred_element_type=jnp.float32)
    sig = jax.nn.sigmoid(gate)
    act = gate * sig
    hidden = (act * up).astype(jnp.bfloat16)
    back = jnp.einsum("esd,efd->esf", dys, w_down, preferred_element_type=jnp.float32)
    route_part = jnp.sum(hidden.astype(jnp.float32) * back, axis=2)
    grad_hidden = weights[:, :, None] * back
    scaled = (weights[:, :, None] * dys.astype(jnp.float32)).astype(jnp.bfloat16)
    grad_down = jnp.einsum("esf,esd->efd", hidden, scaled, preferred_element_type=jnp.float32)
    d_gate = (grad_hidden * up * sig * (1.0 + gate * (1.0 - sig))).astype(jnp.bfloat16)
    d_up = (grad_hidden * act).astype(jnp.bfloat16)
    grad_gate = jnp.einsum("esf,esd->efd", d_gate, xs, preferred_element_type=jnp.float32)
    grad_up = jnp.einsum("esf,esd->efd", d_up, xs, preferred_element_type=jnp.float32)
    partial_value = jnp.einsum("esf,efd->esd", d_gate, w_gate, preferred_element_type=jnp.float32)
    partial_value = partial_value + jnp.einsum(
        "esf,efd->esd", d_up, w_up, preferred_element_type=jnp.float32
    )
    route_total = lax.psum(route_part, "hidden")
    route_back = from_local(route_total, n_groups, capacity)
    summed = lax.psum_scatter(
        partial_value.astype(jnp.bfloat16), "hidden", scatter_dimension=2, tiled=True
    ).astype(jnp.float32)
    back_rows, back_route = (
        lax.all_to_all(
            from_local(summed, n_groups, capacity).astype(jnp.bfloat16),
            "expert",
            split_axis=0,
            concat_axis=0,
            tiled=True,
        ).astype(jnp.float32),
        lax.all_to_all(
            route_back.astype(jnp.bfloat16), "expert", split_axis=0, concat_axis=0, tiled=True
        ).astype(route_back.dtype),
    )
    per_pair = back_rows.reshape(experts * capacity, back_rows.shape[2])[dest]
    grad_input = jnp.sum(per_pair.reshape(tok_count, top, per_pair.shape[1]), axis=1).astype(
        jnp.bfloat16
    )
    grad_route = back_route.reshape(-1)[dest].reshape(tok_count, top)
    return (grad_input, grad_route, grad_gate, grad_up, grad_down)


MESH = pl.DeviceIdType.MESH
F32 = jnp.float32
BF16 = jnp.bfloat16


def places():
    e, h = lax.axis_index("expert"), lax.axis_index("hidden")
    core, z = e % 2, e // 2
    x, y = h % 2, h // 2
    across_x = (e, y * 2 + (1 - x))
    across_y = (e, (1 - y) * 2 + x)
    sibling = (z * 2 + (1 - core), h)
    return e, h, z, core, x, y, across_x, across_y, sibling


def greet(n_expert, e, h, across_x, across_y):
    barrier = pltpu.get_barrier_semaphore()
    peers = [((e + i) % n_expert, h) for i in range(1, n_expert)] + [across_x, across_y]
    for peer in peers:
        pl.semaphore_signal(barrier, inc=1, device_id=peer, device_id_type=MESH)
    pl.semaphore_wait(barrier, len(peers))


def send(src, dst, send_sem, recv_sem, device):
    return pltpu.make_async_remote_copy(
        src_ref=src, dst_ref=dst, send_sem=send_sem, recv_sem=recv_sem,
        device_id=device, device_id_type=MESH,
    )


def rows_of(meta, e, capacity):
    top = meta.shape[0] // 2
    count = meta.shape[1]
    hits = (meta[:top] == e.astype(F32)).astype(F32)
    named = jnp.sum(hits, axis=0, keepdims=True)
    weight = jnp.sum(hits * meta[top:], axis=0, keepdims=True)
    before = (
        lax.broadcasted_iota(jnp.int32, (count, count), 0)
        < lax.broadcasted_iota(jnp.int32, (count, count), 1)
    ).astype(F32).astype(BF16)
    place = jnp.dot(
        jnp.broadcast_to(named, (16, count)).astype(BF16), before, preferred_element_type=F32
    )[:1]
    place = jnp.where(named > 0.5, place, -1.0)
    slots = lax.broadcasted_iota(jnp.int32, (capacity, count), 0).astype(F32)
    onehot = (slots == place).astype(F32)
    return onehot, hits, jnp.sum(onehot * weight, axis=1, keepdims=True)


def fused_kernel(
    n_expert, capacity, x_ref, dy_ref, meta_ref, wg_hbm, wu_hbm, wd_hbm,
    xs_out, dys_out, hidden_out, dg_out, du_out, grad_out, route_out,
    gx, gd, gm, wg, wu, wd, xs, dys, hid, dgs, dus, tok,
    got_a, sum_a, got_bx, got_by, sum_bx, sum_by, got_c, sum_c, got_d,
    route, route_x, route_s, route_y, route_t, route_z,
    own_sem, zs, zr, xsem, xr, ysem, yr, ds, dr, ss, sr, ms, mr, w_sem, o_sem,
    sa, ra, sbx, rbx, sby, rby, sc, rc, sd, rd, sroute, rroute, srx, rrx,
):
    nz = n_expert // 2
    count, width = x_ref.shape
    half = count // 2
    shares = gx.shape[1]
    rows = 2 * capacity
    e, h, z, core, x, y, across_x, across_y, sibling = places()
    hx, hy, hd = across_x[1], across_y[1], (1 - y) * 2 + (1 - x)
    load = [
        pltpu.make_async_copy(src, dst, w_sem.at[i])
        for i, (src, dst) in enumerate(((wg_hbm, wg), (wu_hbm, wu), (wd_hbm, wd)))
    ]
    for copy in load:
        copy.start()
    greet(n_expert, e, h, across_x, across_y)
    full = (x_ref, dy_ref)
    out = (gx, gd)
    own = [pltpu.make_async_copy(full[t], out[t].at[e, h], own_sem.at[t]) for t in range(2)]
    own.append(pltpu.make_async_copy(meta_ref, gm.at[e], own_sem.at[2]))
    for copy in own:
        copy.start()

    def arrived(slot, send_sem, recv_sem, device):
        send(slot, slot, send_sem, recv_sem, device).wait_recv()

    def meta_to(i):
        return send(meta_ref, gm.at[e], ms.at[i], mr.at[i], ((e + n_expert - i) % n_expert, h))

    def column(j):
        return ((z + j) % nz) * 2 + core

    def z_send(t, i):
        to = ((z + nz - i) % nz) * 2 + core
        return send(full[t], out[t].at[e, h], zs.at[t, i], zr.at[t, i], (to, h))

    def first_sends(t, j, src):
        slot = out[t].at[column(j), h]
        src = slot if src is None else src
        return [
            send(src, slot, xsem.at[t, j], xr.at[t, j], across_x),
            send(src, slot, ysem.at[t, j], yr.at[t, j], across_y),
            send(src, slot, ss.at[t, j, 0], sr.at[t, j, 0], sibling),
        ]

    def second_sends(t, j, side):
        if side == 0:
            slot = out[t].at[column(j), hx]
            part = slot.at[pl.ds(0, half)]
            to = across_y
        else:
            slot = out[t].at[column(j), hy]
            part = slot.at[pl.ds(half, half)]
            to = across_x
        return [
            send(part, part, ds.at[t, j, side], dr.at[t, j, side], to),
            send(slot, slot, ss.at[t, j, 1 + side], sr.at[t, j, 1 + side], sibling),
        ]

    def third_sends(t, j):
        slot = out[t].at[column(j), hd]
        return [send(slot, slot, ss.at[t, j, 3], sr.at[t, j, 3], sibling)]

    def start(copies):
        for copy in copies:
            copy.start()

    def first(t, j):
        arrived(out[t].at[column(j), h], zs.at[t, j], zr.at[t, j], across_x)
        start(first_sends(t, j, None))

    def second(t, j):
        arrived(out[t].at[column(j), hx], xsem.at[t, j], xr.at[t, j], across_x)
        start(second_sends(t, j, 0))
        arrived(out[t].at[column(j), hy], ysem.at[t, j], yr.at[t, j], across_y)
        start(second_sends(t, j, 1))

    def third(t, j):
        slot = out[t].at[column(j), hd]
        for k in range(2):
            part = slot.at[pl.ds(k * half, half)]
            arrived(part, ds.at[t, j, k], dr.at[t, j, k], across_y)
        start(third_sends(t, j))

    def from_sibling(t, j):
        b = ((z + j) % nz) * 2 + (1 - core)
        for k, part in enumerate((h, hx, hy, hd)):
            arrived(out[t].at[b, part], ss.at[t, j, k], sr.at[t, j, k], sibling)

    start(first_sends(0, 0, x_ref))
    start([meta_to(i) for i in range(1, n_expert)])
    start(first_sends(1, 0, dy_ref))
    for i in range(1, nz):
        for t in range(2):
            z_send(t, i).start()
    second(0, 0)
    first(0, 1)
    second(1, 0)
    third(0, 0)
    first(1, 1)
    third(1, 0)
    for copy in load + own:
        copy.wait()
    for i in range(1, n_expert):
        arrived(gm.at[(e + i) % n_expert], ms.at[i], mr.at[i], sibling)
    turned = (((1,), (1,)), ((), ()))

    def kept(j):
        at = pl.ds(pl.multiple_of(j * rows, 32), rows)
        return (
            pltpu.make_async_copy(xs, xs_out.at[at], o_sem.at[0]),
            pltpu.make_async_copy(dys, dys_out.at[at], o_sem.at[1]),
            pltpu.make_async_copy(hid, hidden_out.at[at], o_sem.at[2]),
            pltpu.make_async_copy(dgs, dg_out.at[at], o_sem.at[3]),
            pltpu.make_async_copy(dus, du_out.at[at], o_sem.at[4]),
        )

    low, high = pl.ds(0, half), pl.ds(half, half)

    def when(condition, action):
        if isinstance(condition, bool):
            if condition:
                action()
        else:
            pl.when(condition)(action)

    def add(a, b):
        return (a.astype(F32) + b.astype(F32)).astype(BF16)

    def a_send(j):
        return send(tok.at[1 - core], got_a.at[j], sa.at[j], ra.at[j], sibling)

    def b_sends(j):
        at = j % 2
        return [
            send(sum_a.at[at, k * 2 + (1 - x), low], got_bx.at[j, k], sbx.at[j, k], rbx.at[j, k], across_x)
            for k in range(2)
        ] + [
            send(sum_a.at[at, (1 - y) * 2 + k, high], got_by.at[j, k], sby.at[j, k], rby.at[j, k], across_y)
            for k in range(2)
        ]

    def c_sends(j):
        at = j % 2
        return [
            send(sum_bx.at[at, 1 - y], got_c.at[j, low], sc.at[j, 0], rc.at[j, 0], across_y),
            send(sum_by.at[at, 1 - x], got_c.at[j, high], sc.at[j, 1], rc.at[j, 1], across_x),
        ]

    def d_send(j):
        to = ((z + j) % nz) * 2 + core
        return send(sum_c.at[j], got_d.at[j], sd.at[j], rd.at[j], (to, h))

    def sent(copies):
        for copy in copies:
            copy.wait_send()

    def stage_b(j):
        a_send(j).wait_recv()
        when(j >= 2, lambda: sent(b_sends(j - 2)))
        for s in range(shares):
            sum_a[j % 2, s] = add(tok[core, s], got_a[j, s])
        start(b_sends(j))

    def stage_c(j):
        when(j >= 2, lambda: sent(c_sends(j - 2)))
        at = j % 2
        copies = b_sends(j)
        for k in range(2):
            copies[k].wait_recv()
            sum_bx[at, k] = add(sum_a[at, k * 2 + x, low], got_bx[j, k])
            copies[2 + k].wait_recv()
            sum_by[at, k] = add(sum_a[at, y * 2 + k, high], got_by[j, k])
        start(c_sends(j))

    def stage_d(j):
        at = j % 2
        for copy in c_sends(j):
            copy.wait_recv()
        sum_c[j, low] = add(sum_bx[at, y], got_c[j, low])
        sum_c[j, high] = add(sum_by[at, x], got_c[j, high])
        when(j >= 1, lambda: d_send(j).start())

    def step(j, carry):
        more, further = j + 1 < nz, j + 2 < nz
        from_sibling(0, j)
        from_sibling(1, j)

        @pl.when(j > 0)
        def _():
            for copy in kept(j)[:2]:
                copy.wait()

        weights, hots = [], []
        for c in range(2):
            b = ((z + j) % nz) * 2 + c
            onehot, hits, weight = rows_of(gm[b], e, capacity)
            hot = onehot.astype(BF16)
            hots.append((onehot, hits))
            weights.append(weight)
            at = pl.ds(c * capacity, capacity)
            for s in range(shares):
                to = pl.ds(s * width, width)
                xs[at, to] = jnp.dot(hot, gx[b, s], preferred_element_type=F32).astype(BF16)
                row = jnp.dot(hot, gd[b, s], preferred_element_type=F32)
                dys[at, to] = row.astype(BF16)
        start(kept(j)[:2])
        weight = jnp.concatenate(weights, axis=0)

        @pl.when(more)
        def _():
            second(0, j + 1)

        @pl.when(j >= 1)
        def _():
            stage_b(j - 1)

        @pl.when(j >= 2)
        def _():
            stage_d(j - 2)

        gate = lax.dot_general(xs[...], wg[...], turned, preferred_element_type=F32)
        up = lax.dot_general(xs[...], wu[...], turned, preferred_element_type=F32)

        @pl.when(more)
        def _():
            third(0, j + 1)
            second(1, j + 1)

        @pl.when(further)
        def _():
            first(0, j + 2)

        back = lax.dot_general(dys[...], wd[...], turned, preferred_element_type=F32)

        @pl.when(j > 0)
        def _():
            for copy in kept(j)[2:5]:
                copy.wait()

        sig = jax.nn.sigmoid(gate)
        act = gate * sig
        hidden = act * up
        hid[...] = (weight * hidden).astype(BF16)
        hidden = hidden.astype(BF16)
        parted = jnp.sum(hidden.astype(F32) * back, axis=1, keepdims=True)
        grad_hidden = weight * back
        dgs[...] = (grad_hidden * up * sig * (1.0 + gate * (1.0 - sig))).astype(BF16)
        dus[...] = (grad_hidden * act).astype(BF16)
        start(kept(j)[2:5])

        @pl.when(more)
        def _():
            third(1, j + 1)

        @pl.when(further)
        def _():
            first(1, j + 2)

        @pl.when(j >= 1)
        def _():
            stage_c(j - 1)
            sent([a_send(j - 1)])

        for c in range(2):
            b = ((z + j) % nz) * 2 + c
            onehot, hits = hots[c]
            at = slice(c * capacity, (c + 1) * capacity)
            row_grad = (
                jnp.dot(dgs[at], wg[...], preferred_element_type=F32)
                + jnp.dot(dus[at], wu[...], preferred_element_type=F32)
            ).astype(BF16)
            token = jnp.dot(onehot.T.astype(BF16), row_grad, preferred_element_type=F32).astype(BF16)
            for s in range(shares):
                tok[c, s] = token[:, s * width : (s + 1) * width]
            per_token = jnp.sum(onehot * parted[at], axis=0, keepdims=True)
            top = hits.shape[0]
            route[b, :top] = hits * per_token
            route[b, top:] = jnp.zeros_like(hits)
        a_send(j).start()
        return carry

    lax.fori_loop(0, nz, step, 0)
    last = nz - 1
    rx = send(route, route_x, srx.at[0], rrx.at[0], across_x)
    rx.start()
    if last >= 1:
        stage_d(last - 1)
    stage_b(last)
    rx.wait_recv()
    route_s[...] = route[...] + route_x[...]
    ry = send(route_s, route_y, srx.at[1], rrx.at[1], across_y)
    ry.start()
    stage_c(last)
    ry.wait_recv()
    route_t[...] = route_s[...] + route_y[...]
    routes = [
        send(route_t.at[(e + i) % n_expert], route_z.at[i], sroute.at[i], rroute.at[i], ((e + i) % n_expert, h))
        for i in range(1, n_expert)
    ]
    start(routes)
    stage_d(last)
    total = route_t[e]
    for i in range(1, n_expert):
        routes[i - 1].wait_recv()
        total = total + route_z[i]
    route_out[...] = total
    total = sum_c[0].astype(F32)
    for j in range(1, nz):
        d_send(j).wait_recv()
        total = total + got_d[j].astype(F32)
    grad_out[...] = total.astype(BF16)
    for copy in kept(last):
        copy.wait()
    sent([a_send(last), rx, ry] + routes + [d_send(j) for j in range(1, nz)])
    for j in range(max(0, nz - 2), nz):
        sent(b_sends(j) + c_sends(j))
    for i in range(1, n_expert):
        meta_to(i).wait_send()
    for t in range(2):
        for j in range(nz):
            if j:
                z_send(t, j).wait_send()
            for copy in first_sends(t, j, full[t] if j == 0 else None):
                copy.wait_send()
            for copy in second_sends(t, j, 0) + second_sends(t, j, 1) + third_sends(t, j):
                copy.wait_send()


def gather_and_expert(x, dy, meta, w_gate, w_up, w_down, n_expert, capacity):
    nz = n_expert // 2
    count, width = x.shape
    hidden, depth = w_gate.shape
    total = n_expert * capacity
    rows = 2 * capacity
    half = count // 2
    dma = pltpu.SemaphoreType.DMA
    vmem = pl.BlockSpec(memory_space=pltpu.VMEM)
    hbm = pl.BlockSpec(memory_space=pl.ANY)

    def room(*shape):
        return pltpu.VMEM(shape, BF16)

    return pl.pallas_call(
        functools.partial(fused_kernel, n_expert, capacity),
        out_shape=(
            jax.ShapeDtypeStruct((total, depth), BF16),
            jax.ShapeDtypeStruct((total, depth), BF16),
            jax.ShapeDtypeStruct((total, hidden), BF16),
            jax.ShapeDtypeStruct((total, hidden), BF16),
            jax.ShapeDtypeStruct((total, hidden), BF16),
            jax.ShapeDtypeStruct((count, width), BF16),
            jax.ShapeDtypeStruct(meta.shape, F32),
        ),
        in_specs=[vmem] * 3 + [hbm] * 3,
        out_specs=[hbm] * 5 + [vmem] * 2,
        scratch_shapes=[
            room(n_expert, 4, count, width),
            room(n_expert, 4, count, width),
            pltpu.VMEM((n_expert,) + meta.shape, F32),
            room(hidden, depth),
            room(hidden, depth),
            room(hidden, depth),
            room(rows, depth),
            room(rows, depth),
            room(rows, hidden),
            room(rows, hidden),
            room(rows, hidden),
            room(2, 4, count, width),
            room(nz, 4, count, width),
            room(2, 4, count, width),
            room(nz, 2, half, width),
            room(nz, 2, half, width),
            room(2, 2, half, width),
            room(2, 2, half, width),
            room(nz, count, width),
            room(nz, count, width),
            room(nz, count, width),
        ]
        + [pltpu.VMEM((n_expert,) + meta.shape, F32)] * 6
        + [
            dma((3,)),
        ]
        + [dma((2, nz))] * 6
        + [dma((2, nz, 2))] * 2
        + [dma((2, nz, 4))] * 2
        + [dma((n_expert,))] * 2
        + [dma((3,)), dma((5,))]
        + [dma((nz,))] * 2
        + [dma((nz, 2))] * 6
        + [dma((nz,))] * 2
        + [dma((n_expert,))] * 2
        + [dma((2,))] * 2,
        compiler_params=pltpu.CompilerParams(
            collective_id=0, has_side_effects=True, vmem_limit_bytes=63 * 1024 * 1024
        ),
    )(x, dy, meta, w_gate, w_up, w_down)


def paired_device(inputs, out_grad, expert_ids, route_weight, w_gate, w_up, w_down):
    n_expert = lax.axis_size("expert")
    local_count = w_gate.shape[0]
    experts = local_count * n_expert
    tok_count, top = expert_ids.shape
    capacity = 3 * top * tok_count // (2 * experts)
    meta = jnp.concatenate([expert_ids.astype(F32).T, route_weight.T], axis=0)
    xs, dys, hidden, dg, du, grad_input, grad_route = gather_and_expert(
        inputs, out_grad, meta, w_gate[0], w_up[0], w_down[0], n_expert, capacity
    )

    def outer(a, b):
        return jnp.einsum("sf,sd->fd", a, b, preferred_element_type=F32)[None]

    return (grad_input, grad_route[:top].T, outer(dg, xs), outer(du, xs), outer(hidden, dys))


def solution(mesh):
    placed = (
        P("expert", "hidden"),
        P("expert", "hidden"),
        P("expert", None),
        P("expert", None),
        P("expert", "hidden", None),
        P("expert", "hidden", None),
        P("expert", "hidden", None),
    )
    return jax.shard_map(
        paired_device if mesh.shape["hidden"] == 4 else plain_device,
        mesh=mesh,
        in_specs=placed,
        out_specs=(
            P("expert", "hidden"),
            P("expert", None),
            P("expert", "hidden", None),
            P("expert", "hidden", None),
            P("expert", "hidden", None),
        ),
        check_vma=False,
    )
```

profile of v0, /device:TPU:0, one launch (start us, length us, event | category | flops | bytes accessed | tf_op | source)
XLA Modules:
  0.0 194.4 jit_solution(3316766501899162351)
XLA Ops:
  0.6 0.7 convert_bitcast_fusion
  1.3 1.3 pad_maximum_fusion.meta_ref
  2.6 162.4 %shard_map.110 = (bf16[1152,2880]{1,0:T(8,128)(2,1)}, bf16[1152,2880]{1,0:T(8,128)(2,1)}, bf16[1152,720]{1,0:T(8,128)(2,1)}, bf16[1152,720]{1,0:T(8,128)(2,1)}, ...) custom-call(bf16[192,720]{1,0:T(8,128)(2,1)} %x_ref.1, bf16[192,720]{1,0:T(8,128)(2,1)} %dy_ref.1, ...), custom_call_target="tpu_custom_call" | custom-call | tf_op jit(solution)/shard_map/pallas_call | solution.py:513
  165.0 1.3 slice_bitcast_fusion
  166.3 0.0 copy-start.1
  166.3 0.0 copy-start.3
  166.3 0.0 slice-start
  166.3 11.0 %convolution_bitcast_fusion.2 = f32[1,720,2880]{2,1,0:T(8,128)} fusion(bf16[1152,720]{1,0:T(8,128)(2,1)} %get-tuple-element.14, bf16[1152,2880]{1,0:T(8,128)(2,1)} %get-tuple-element.15), kind=kOutput, calls=%fused_computation.2 | convolution fusion | flops 4777574400 | bytes 16588800 | tf_op jit(solution)/shard_map/sf,sd->fd/dot_general | solution.py:581
  177.3 0.0 copy-done.1
  177.3 0.0 copy-done.3
  177.3 0.0 slice-start.1
  177.3 0.0 copy-start.2
  177.3 8.2 %convolution_bitcast_fusion.1 = f32[1,720,2880]{2,1,0:T(8,128)} fusion(bf16[1152,720]{1,0:T(8,128)(2,1)S(1)} %copy-done.3, bf16[1152,2880]{1,0:T(8,128)(2,1)S(1)} %copy-done.1), kind=kOutput, calls=%fused_computation.1 | convolution fusion | flops 4777574400 | bytes 16588800 | tf_op jit(solution)/shard_map/sf,sd->fd/dot_general | solution.py:581
  185.5 0.0 slice-done
  185.5 0.0 slice-done.1
  185.5 0.0 copy-done.2
  185.5 0.0 copy-start
  185.5 8.2 %convolution_bitcast_fusion = f32[1,720,2880]{2,1,0:T(8,128)} fusion(bf16[1152,720]{1,0:T(8,128)(2,1)S(1)} %copy-done.2, bf16[1152,2880]{1,0:T(8,128)(2,1)S(1)} %bitcast.25), kind=kOutput, calls=%fused_computation | convolution fusion | flops 4777574400 | bytes 16588800 | tf_op jit(solution)/shard_map/sf,sd->fd/dot_general | solution.py:581
  193.7 0.0 copy-done
  193.7 0.7 copy.13
  (1 shorter events, 0.0 us)
Async XLA Ops:
  166.3 11.0 %copy-start.1 = (bf16[1152,2880]{1,0:T(8,128)(2,1)S(1)}, bf16[1152,2880]{1,0:T(8,128)(2,1)}, u32[]{:S(2)}) copy-start(bf16[1152,2880]{1,0:T(8,128)(2,1)} %get-tuple-element.15) | copy-start | bytes 19906564
  166.3 11.0 %copy-start.3 = (bf16[1152,720]{1,0:T(8,128)(2,1)S(1)}, bf16[1152,720]{1,0:T(8,128)(2,1)}, u32[]{:S(2)}) copy-start(bf16[1152,720]{1,0:T(8,128)(2,1)} %get-tuple-element.16) | copy-start | bytes 4976644
  166.3 19.2 %slice-start = ((s8[6782976]{0:T(1024)(128)(4,1)}), s8[4194304]{0:T(1024)(128)(4,1)S(1)}, s32[]{:S(2)}) async-start(s8[6782976]{0:T(1024)(128)(4,1)} %bitcast.24), calls=%async_computation | async-start | bytes 8388608
  177.3 8.2 %slice-start.1 = ((s8[6782976]{0:T(1024)(128)(4,1)}), s8[2588672]{0:T(1024)(128)(4,1)S(1)}, s32[]{:S(2)}) async-start(s8[6782976]{0:T(1024)(128)(4,1)} %bitcast.24), calls=%async_computation.1 | async-start | bytes 5177344
  177.3 8.2 %copy-start.2 = (bf16[1152,720]{1,0:T(8,128)(2,1)S(1)}, bf16[1152,720]{1,0:T(8,128)(2,1)}, u32[]{:S(2)}) copy-start(bf16[1152,720]{1,0:T(8,128)(2,1)} %get-tuple-element.17) | copy-start | bytes 4976644
  185.5 8.2 %copy-start = (bf16[192,720]{1,0:T(8,128)(2,1)S(1)}, bf16[192,720]{1,0:T(8,128)(2,1)}, u32[]{:S(2)}) copy-start(bf16[192,720]{1,0:T(8,128)(2,1)} %get-tuple-element.24) | copy-start | bytes 829444
where the time goes:
time: 195 us; the launch traced here: 194 us
  Pallas kernels  162 us (83%)
  matrix products  27.3 us (14%)
  local copies, waits for them, and re-layouts  2.03 us (1%)
  other arithmetic  1.98 us (1%)
    pallas_call x1, Pallas kernels, gather_and_expert(): pl.pallas_call(functools.partial(fused_kernel, n_expert, capacity), out_s...  162 us
    dot_general x3, matrix products, outer(): return jnp.einsum('sf,sd->fd', a, b, preferred_element_type=F32)[None]  27.3 us

commit v1 on v0

v1 whole, which is shorter than its diff:
```python
import functools

import jax
import jax.numpy as jnp
from jax import lax
from jax.experimental import pallas as pl
from jax.experimental.pallas import tpu as pltpu
from jax.sharding import PartitionSpec as P


def slot_tables(expert_ids, experts, capacity):
    count, top = expert_ids.shape
    flat = expert_ids.reshape(-1)
    onehot = (flat[:, None] == jnp.arange(experts, dtype=jnp.int32)[None, :]).astype(jnp.int32)
    position = jnp.cumsum(onehot, axis=0) - 1
    slot = jnp.sum(onehot * position, axis=1)
    dest = flat * capacity + slot
    table = (
        jnp.zeros((experts * capacity,), jnp.int32)
        .at[dest]
        .set(jnp.arange(count * top, dtype=jnp.int32))
    )
    filled = jnp.zeros((experts * capacity,), jnp.int32).at[dest].set(1)
    return (dest, table, filled)


def pack_rows(values, table, filled, top, experts, capacity):
    picked = values[table // top] * filled.astype(values.dtype)[:, None]
    return picked.reshape(experts, capacity, values.shape[1])


def to_local(buffer, n_groups, local_count):
    rest = buffer.shape[2:]
    shaped = buffer.reshape((n_groups, local_count, buffer.shape[1]) + rest)
    return jnp.swapaxes(shaped, 0, 1).reshape((local_count, n_groups * buffer.shape[1]) + rest)


def from_local(buffer, n_groups, capacity):
    local_count = buffer.shape[0]
    rest = buffer.shape[2:]
    shaped = buffer.reshape((local_count, n_groups, capacity) + rest)
    return jnp.swapaxes(shaped, 0, 1).reshape((n_groups * local_count, capacity) + rest)


def plain_device(inputs, out_grad, expert_ids, route_weight, w_gate, w_up, w_down):
    n_groups = lax.axis_size("expert")
    local_count = w_gate.shape[0]
    experts = local_count * n_groups
    tok_count, top = expert_ids.shape
    capacity = 3 * top * tok_count // (2 * experts)
    dest, table, filled = slot_tables(expert_ids, experts, capacity)
    send_weight = (route_weight.reshape(-1)[table] * filled.astype(jnp.float32)).reshape(
        experts, capacity
    )
    send_x = pack_rows(inputs, table, filled, top, experts, capacity)
    send_dy = pack_rows(out_grad, table, filled, top, experts, capacity)
    got_x, got_dy, got_weight = (
        lax.all_to_all(send_x, "expert", split_axis=0, concat_axis=0, tiled=True),
        lax.all_to_all(send_dy, "expert", split_axis=0, concat_axis=0, tiled=True),
        lax.all_to_all(
            send_weight.astype(jnp.bfloat16), "expert", split_axis=0, concat_axis=0, tiled=True
        ).astype(send_weight.dtype),
    )
    rows_x, rows_dy = (
        lax.all_gather(got_x, "hidden", axis=2, tiled=True),
        lax.all_gather(got_dy, "hidden", axis=2, tiled=True),
    )
    xs = to_local(rows_x, n_groups, local_count)
    dys = to_local(rows_dy, n_groups, local_count)
    weights = to_local(got_weight, n_groups, local_count)
    gate = jnp.einsum("esd,efd->esf", xs, w_gate, preferred_element_type=jnp.float32)
    up = jnp.einsum("esd,efd->esf", xs, w_up, preferred_element_type=jnp.float32)
    sig = jax.nn.sigmoid(gate)
    act = gate * sig
    hidden = (act * up).astype(jnp.bfloat16)
    back = jnp.einsum("esd,efd->esf", dys, w_down, preferred_element_type=jnp.float32)
    route_part = jnp.sum(hidden.astype(jnp.float32) * back, axis=2)
    grad_hidden = weights[:, :, None] * back
    scaled = (weights[:, :, None] * dys.astype(jnp.float32)).astype(jnp.bfloat16)
    grad_down = jnp.einsum("esf,esd->efd", hidden, scaled, preferred_element_type=jnp.float32)
    d_gate = (grad_hidden * up * sig * (1.0 + gate * (1.0 - sig))).astype(jnp.bfloat16)
    d_up = (grad_hidden * act).astype(jnp.bfloat16)
    grad_gate = jnp.einsum("esf,esd->efd", d_gate, xs, preferred_element_type=jnp.float32)
    grad_up = jnp.einsum("esf,esd->efd", d_up, xs, preferred_element_type=jnp.float32)
    partial_value = jnp.einsum("esf,efd->esd", d_gate, w_gate, preferred_element_type=jnp.float32)
    partial_value = partial_value + jnp.einsum(
        "esf,efd->esd", d_up, w_up, preferred_element_type=jnp.float32
    )
    route_total = lax.psum(route_part, "hidden")
    route_back = from_local(route_total, n_groups, capacity)
    summed = lax.psum_scatter(
        partial_value.astype(jnp.bfloat16), "hidden", scatter_dimension=2, tiled=True
    ).astype(jnp.float32)
    back_rows, back_route = (
        lax.all_to_all(
            from_local(summed, n_groups, capacity).astype(jnp.bfloat16),
            "expert",
            split_axis=0,
            concat_axis=0,
            tiled=True,
        ).astype(jnp.float32),
        lax.all_to_all(
            route_back.astype(jnp.bfloat16), "expert", split_axis=0, concat_axis=0, tiled=True
        ).astype(route_back.dtype),
    )
    per_pair = back_rows.reshape(experts * capacity, back_rows.shape[2])[dest]
    grad_input = jnp.sum(per_pair.reshape(tok_count, top, per_pair.shape[1]), axis=1).astype(
        jnp.bfloat16
    )
    grad_route = back_route.reshape(-1)[dest].reshape(tok_count, top)
    return (grad_input, grad_route, grad_gate, grad_up, grad_down)


MESH = pl.DeviceIdType.MESH
F32 = jnp.float32
BF16 = jnp.bfloat16


def places():
    e, h = lax.axis_index("expert"), lax.axis_index("hidden")
    core, z = e % 2, e // 2
    x, y = h % 2, h // 2
    across_x = (e, y * 2 + (1 - x))
    across_y = (e, (1 - y) * 2 + x)
    sibling = (z * 2 + (1 - core), h)
    return e, h, z, core, x, y, across_x, across_y, sibling


def flip(z, j):
    low = z % 2 + j % 2 - 2 * (z % 2) * (j % 2)
    high = z // 2 + j // 2 - 2 * (z // 2) * (j // 2)
    return low + 2 * high


def greet(n_expert, e, h, across_x, across_y):
    barrier = pltpu.get_barrier_semaphore()
    peers = [((e + i) % n_expert, h) for i in range(1, n_expert)] + [across_x, across_y]
    for peer in peers:
        pl.semaphore_signal(barrier, inc=1, device_id=peer, device_id_type=MESH)
    pl.semaphore_wait(barrier, len(peers))


def send(src, dst, send_sem, recv_sem, device):
    return pltpu.make_async_remote_copy(
        src_ref=src, dst_ref=dst, send_sem=send_sem, recv_sem=recv_sem,
        device_id=device, device_id_type=MESH,
    )


def routed(meta, e):
    top = meta.shape[0] // 2
    hits = (meta[:top] == e.astype(F32)).astype(F32)
    return hits, jnp.sum(hits * meta[top:], axis=0, keepdims=True)


def diagonal(count):
    return (
        lax.broadcasted_iota(jnp.int32, (count, count), 0)
        == lax.broadcasted_iota(jnp.int32, (count, count), 1)
    ).astype(F32)


def fused_kernel(
    n_expert, x_ref, dy_ref, meta_ref, wg_hbm, wu_hbm, wd_hbm,
    w, grad_out, route_out,
    g, gm, d, tok, got_a, got_bx, got_by, got_c, got_d,
    route, route_x, route_s, route_y, route_t, route_z,
    own_sem, zs, zr, xsem, xr, ysem, yr, ds, dr, ss, sr, ms, mr, w_sem,
    sa, ra, sbx, rbx, sby, rby, sc, rc, sd, rd, sroute, rroute, srx, rrx,
):
    nz = n_expert // 2
    last = nz - 1
    count, width = x_ref.shape
    half = count // 2
    shares = g.shape[1]
    e, h, z, core, x, y, across_x, across_y, sibling = places()
    hx, hy, hd = across_x[1], across_y[1], (1 - y) * 2 + (1 - x)
    load = [
        pltpu.make_async_copy(src, w.at[i], w_sem.at[i])
        for i, src in enumerate((wg_hbm, wu_hbm, wd_hbm))
    ]
    for copy in load:
        copy.start()
    greet(n_expert, e, h, across_x, across_y)
    full = (x_ref, dy_ref)

    def block(t, b, share, start=0, size=count):
        return g.at[t, share, pl.ds(pl.multiple_of(b * count + start, 32), size)]

    own = [pltpu.make_async_copy(full[t], block(t, e, h), own_sem.at[t]) for t in range(2)]
    own.append(pltpu.make_async_copy(meta_ref, gm.at[e], own_sem.at[2]))

    def arrived(slot, send_sem, recv_sem, device):
        send(slot, slot, send_sem, recv_sem, device).wait_recv()

    def meta_to(i):
        return send(meta_ref, gm.at[e], ms.at[i], mr.at[i], ((e + n_expert - i) % n_expert, h))

    def column(j):
        return flip(z, j) * 2 + core

    def z_send(t, i):
        return send(full[t], block(t, e, h), zs.at[t, i], zr.at[t, i], (column(i), h))

    def first_sends(t, j, src):
        slot = block(t, column(j), h)
        src = slot if src is None else src
        return [
            send(src, slot, xsem.at[t, j], xr.at[t, j], across_x),
            send(src, slot, ysem.at[t, j], yr.at[t, j], across_y),
            send(src, slot, ss.at[t, j, 0], sr.at[t, j, 0], sibling),
        ]

    def second_sends(t, j, side):
        share, to = ((hx, across_y), (hy, across_x))[side]
        slot = block(t, column(j), share)
        part = block(t, column(j), share, side * half, half)
        return [
            send(part, part, ds.at[t, j, side], dr.at[t, j, side], to),
            send(slot, slot, ss.at[t, j, 1 + side], sr.at[t, j, 1 + side], sibling),
        ]

    def third_sends(t, j):
        slot = block(t, column(j), hd)
        return [send(slot, slot, ss.at[t, j, 3], sr.at[t, j, 3], sibling)]

    def start(copies):
        for copy in copies:
            copy.start()

    def sent(copies):
        for copy in copies:
            copy.wait_send()

    def first(t, j):
        arrived(block(t, column(j), h), zs.at[t, j], zr.at[t, j], across_x)
        start(first_sends(t, j, None))

    def second(t, j):
        arrived(block(t, column(j), hx), xsem.at[t, j], xr.at[t, j], across_x)
        start(second_sends(t, j, 0))
        arrived(block(t, column(j), hy), ysem.at[t, j], yr.at[t, j], across_y)
        start(second_sends(t, j, 1))

    def third(t, j):
        for k in range(2):
            arrived(block(t, column(j), hd, k * half, half), ds.at[t, j, k], dr.at[t, j, k], across_y)
        start(third_sends(t, j))

    def from_sibling(t, j):
        b = flip(z, j) * 2 + (1 - core)
        for k, part in enumerate((h, hx, hy, hd)):
            arrived(block(t, b, part), ss.at[t, j, k], sr.at[t, j, k], sibling)

    start(first_sends(0, 0, x_ref))
    start([meta_to(i) for i in range(1, n_expert)])
    for t in range(2):
        z_send(t, 1).start()
    start(first_sends(1, 0, dy_ref))
    start(own)
    second(0, 0)
    first(0, 1)
    z_send(0, 2).start()
    second(1, 0)
    first(1, 1)
    z_send(1, 2).start()
    for i in range(3, nz):
        for t in range(2):
            z_send(t, i).start()
    third(0, 0)
    for copy in load + own:
        copy.wait()
    for i in range(1, n_expert):
        arrived(gm.at[(e + i) % n_expert], ms.at[i], mr.at[i], sibling)

    turned = (((1,), (1,)), ((), ()))
    low, high = pl.ds(0, half), pl.ds(half, half)

    def add(a, b):
        return (a.astype(F32) + b.astype(F32)).astype(BF16)

    def a_send(j):
        return send(tok.at[1 - core], got_a.at[j], sa.at[j], ra.at[j], sibling)

    def b_sends(j):
        return [
            send(got_a.at[j, k * 2 + (1 - x), low], got_bx.at[j, k], sbx.at[j, k], rbx.at[j, k], across_x)
            for k in range(2)
        ] + [
            send(got_a.at[j, (1 - y) * 2 + k, high], got_by.at[j, k], sby.at[j, k], rby.at[j, k], across_y)
            for k in range(2)
        ]

    def c_sends(j):
        return [
            send(got_bx.at[j, 1 - y], got_c.at[j, low], sc.at[j, 0], rc.at[j, 0], across_y),
            send(got_by.at[j, 1 - x], got_c.at[j, high], sc.at[j, 1], rc.at[j, 1], across_x),
        ]

    def d_send(j):
        return send(got_c.at[j], got_d.at[j], sd.at[j], rd.at[j], (column(j), h))

    def fold(j):
        a_send(j).wait()
        for s in range(shares):
            got_a[j, s] = add(tok[core, s], got_a[j, s])

    def stage_b(j):
        start(b_sends(j))

    def stage_c(j):
        copies = b_sends(j)
        for k in range(2):
            copies[k].wait_recv()
            got_bx[j, k] = add(got_a[j, k * 2 + x, low], got_bx[j, k])
            copies[2 + k].wait_recv()
            got_by[j, k] = add(got_a[j, y * 2 + k, high], got_by[j, k])
        start(c_sends(j))

    def stage_d(j):
        for copy in c_sends(j):
            copy.wait_recv()
        got_c[j, low] = add(got_bx[j, y], got_c[j, low])
        got_c[j, high] = add(got_by[j, x], got_c[j, high])
        if j:
            d_send(j).start()

    rx = send(route, route_x, srx.at[0], rrx.at[0], across_x)
    ry = send(route_s, route_y, srx.at[1], rrx.at[1], across_y)
    routes = [
        send(route_t.at[(e + i) % n_expert], route_z.at[i], sroute.at[i], rroute.at[i], ((e + i) % n_expert, h))
        for i in range(1, n_expert)
    ]

    def at_share(s):
        return pl.ds(s * width, width)

    def project(t, rows, m):
        total = None
        for s in range(shares):
            part = lax.dot_general(
                g[t, s, rows], w[m, :, at_share(s)], turned, preferred_element_type=F32
            )
            total = part if total is None else total + part
        return total

    eye = diagonal(count)

    def step(j, carry):
        more, further, final = j + 1 < nz, j + 2 < nz, j == last
        plane = flip(z, j)
        rows = pl.ds(pl.multiple_of(plane * (2 * count), 64), 2 * count)
        from_sibling(0, j)

        @pl.when(more)
        def _():
            second(0, j + 1)

        @pl.when(final)
        def _():
            for i in range(1, last - 1):
                stage_b(i)

        gate = project(0, rows, 0)
        up = project(0, rows, 1)

        @pl.when(further)
        def _():
            first(0, j + 2)

        @pl.when(j > 0)
        def _():
            fold(j - 1)

        @pl.when(final)
        def _():
            stage_b(last - 1)

        third(1, j)
        from_sibling(1, j)
        back = project(1, rows, 2)
        hits, weights = [], []
        for c in range(2):
            hit, row = routed(gm[plane * 2 + c], e)
            hits.append(hit)
            weights.append(jnp.sum(eye * row, axis=1, keepdims=True))
        weight = jnp.concatenate(weights, axis=0)
        sig = jax.nn.sigmoid(gate)
        act = gate * sig
        hidden = act * up
        d[2, rows] = (weight * hidden).astype(BF16)
        hidden = hidden.astype(BF16)
        parted = jnp.sum(hidden.astype(F32) * back, axis=1, keepdims=True)
        grad_hidden = weight * back
        d[0, rows] = (grad_hidden * up * sig * (1.0 + gate * (1.0 - sig))).astype(BF16)
        d[1, rows] = (grad_hidden * act).astype(BF16)
        for c in range(2):
            per_token = jnp.sum(eye * parted[c * count : (c + 1) * count], axis=0, keepdims=True)
            top = hits[c].shape[0]
            route[plane * 2 + c, :top] = hits[c] * per_token
            route[plane * 2 + c, top:] = jnp.zeros_like(hits[c])

        @pl.when(more)
        def _():
            second(1, j + 1)

        @pl.when(further)
        def _():
            first(1, j + 2)

        @pl.when(more)
        def _():
            third(0, j + 1)

        @pl.when(final)
        def _():
            rx.start()
            for i in range(1, last - 1):
                stage_c(i)

        for s in range(shares):
            row_grad = (
                jnp.dot(d[0, rows], w[0, :, at_share(s)], preferred_element_type=F32)
                + jnp.dot(d[1, rows], w[1, :, at_share(s)], preferred_element_type=F32)
            ).astype(BF16)
            for c in range(2):
                tok[c, s] = row_grad[c * count : (c + 1) * count]
        a_send(j).start()
        return carry

    lax.fori_loop(0, nz, step, 0)

    def route_on():
        rx.wait_recv()
        route_s[...] = route[...] + route_x[...]
        ry.start()

    def route_out_to_owners():
        ry.wait_recv()
        route_t[...] = route_s[...] + route_y[...]
        start(routes)

    def tail_one():
        route_on()
        for i in range(1, last - 1):
            stage_d(i)
        stage_c(last - 1)
        fold(last)
        stage_b(last)
        stage_b(0)

    events = {
        (0, 0): tail_one,
        (0, 2): route_out_to_owners,
        (0, 3): lambda: stage_d(last - 1),
        (1, 1): lambda: stage_c(last),
        (1, 3): lambda: stage_d(last),
        (2, 1): lambda: stage_c(0),
    }

    def outer(m, carry):
        for s in range(shares):
            w[m, :, at_share(s)] = lax.dot_general(
                d[m], g[m // 2, s], (((0,), (0,)), ((), ())), preferred_element_type=F32
            ).astype(BF16)
            for (at_m, at_s), event in events.items():
                if at_s == s:
                    pl.when(m == at_m)(event)
        return carry

    lax.fori_loop(0, 3, outer, 0)
    stage_d(0)
    total = route_t[e]
    for i in range(1, n_expert):
        routes[i - 1].wait_recv()
        total = total + route_z[i]
    route_out[...] = total
    total = got_c[0].astype(F32)
    for j in range(1, nz):
        d_send(j).wait_recv()
        total = total + got_d[j].astype(F32)
    grad_out[...] = total.astype(BF16)
    sent([rx, ry] + routes + [d_send(j) for j in range(1, nz)])
    for j in range(nz):
        sent(b_sends(j) + c_sends(j))
    for i in range(1, n_expert):
        meta_to(i).wait_send()
    for t in range(2):
        for j in range(nz):
            if j:
                z_send(t, j).wait_send()
            sent(first_sends(t, j, full[t] if j == 0 else None))
            sent(second_sends(t, j, 0) + second_sends(t, j, 1) + third_sends(t, j))


def gather_and_expert(x, dy, meta, w_gate, w_up, w_down, n_expert):
    nz = n_expert // 2
    count, width = x.shape
    hidden, depth = w_gate.shape
    total = n_expert * count
    half = count // 2
    dma = pltpu.SemaphoreType.DMA
    vmem = pl.BlockSpec(memory_space=pltpu.VMEM)
    hbm = pl.BlockSpec(memory_space=pl.ANY)

    def room(*shape):
        return pltpu.VMEM(shape, BF16)

    return pl.pallas_call(
        functools.partial(fused_kernel, n_expert),
        out_shape=(
            jax.ShapeDtypeStruct((3, hidden, depth), BF16),
            jax.ShapeDtypeStruct((count, width), BF16),
            jax.ShapeDtypeStruct(meta.shape, F32),
        ),
        in_specs=[vmem] * 3 + [hbm] * 3,
        out_specs=[vmem] * 3,
        scratch_shapes=[
            room(2, 4, total, width),
            pltpu.VMEM((n_expert,) + meta.shape, F32),
            room(3, total, hidden),
            room(2, 4, count, width),
            room(nz, 4, count, width),
            room(nz, 2, half, width),
            room(nz, 2, half, width),
            room(nz, count, width),
            room(nz, count, width),
        ]
        + [pltpu.VMEM((n_expert,) + meta.shape, F32)] * 6
        + [dma((3,))]
        + [dma((2, nz))] * 6
        + [dma((2, nz, 2))] * 2
        + [dma((2, nz, 4))] * 2
        + [dma((n_expert,))] * 2
        + [dma((3,))]
        + [dma((nz,))] * 2
        + [dma((nz, 2))] * 6
        + [dma((nz,))] * 2
        + [dma((n_expert,))] * 2
        + [dma((2,))] * 2,
        compiler_params=pltpu.CompilerParams(
            collective_id=0, has_side_effects=True, vmem_limit_bytes=63 * 1024 * 1024
        ),
    )(x, dy, meta, w_gate, w_up, w_down)


def paired_device(inputs, out_grad, expert_ids, route_weight, w_gate, w_up, w_down):
    top = expert_ids.shape[1]
    meta = jnp.concatenate([expert_ids.astype(F32).T, route_weight.T], axis=0)
    grads, grad_input, grad_route = gather_and_expert(
        inputs, out_grad, meta, w_gate[0], w_up[0], w_down[0], lax.axis_size("expert")
    )
    wide = [grads[i].astype(F32)[None] for i in range(3)]
    return (grad_input, grad_route[:top].T, *wide)


def solution(mesh):
    placed = (
        P("expert", "hidden"),
        P("expert", "hidden"),
        P("expert", None),
        P("expert", None),
        P("expert", "hidden", None),
        P("expert", "hidden", None),
        P("expert", "hidden", None),
    )
    return jax.shard_map(
        paired_device
        if mesh.shape["hidden"] == 4 and mesh.shape["expert"] == 8
        else plain_device,
        mesh=mesh,
        in_specs=placed,
        out_specs=(
            P("expert", "hidden"),
            P("expert", None),
            P("expert", "hidden", None),
            P("expert", "hidden", None),
            P("expert", "hidden", None),
        ),
        check_vma=False,
    )
```

time: 195 us -> 167 us (0.86)
  matrix products: 27.3 us -> 0 us
  Pallas kernels: 162 us -> 150 us
  other arithmetic: 1.98 us -> 13.7 us
    dot_general x3 -> x0, matrix products: 27.3 us -> none  [outer(): return jnp.einsum('sf,sd->fd', a, b, preferred_element_type=F32)[None]]
    pallas_call x1, Pallas kernels: 162 us -> 150 us  [gather_and_expert(): pl.pallas_call(functools.partial(fused_kernel, n_expert), out_shape=(jax....]
    convert_element_type x0 -> x1, other arithmetic: none -> 11.7 us  [paired_device(): wide = [grads[i].astype(F32)[None] for i in range(3)]]
where the time goes in v1:
time: 167 us; the launch traced here: 166 us
  Pallas kernels  150 us (90%)
  other arithmetic  13.7 us (8%)
  local copies, waits for them, and re-layouts  2.01 us (1%)
    pallas_call x1, Pallas kernels, gather_and_expert(): pl.pallas_call(functools.partial(fused_kernel, n_expert), out_shape=(jax....  150 us
    convert_element_type x1, other arithmetic, paired_device(): wide = [grads[i].astype(F32)[None] for i in range(3)]  11.7 us

profile of v1, /device:TPU:0, one launch (start us, length us, event | category | flops | bytes accessed | tf_op | source)
XLA Modules:
  0.0 166.2 jit_solution(11444966606798009997)
XLA Ops:
  0.6 0.7 convert_bitcast_fusion
  1.3 1.3 pad_maximum_fusion.meta_ref
  2.6 149.9 %shard_map.110 = (bf16[3,720,2880]{2,1,0:T(8,128)(2,1)}, bf16[192,720]{1,0:T(8,128)(2,1)}, f32[8,192]{1,0:T(8,128)}) custom-call(bf16[192,720]{1,0:T(8,128)(2,1)} %x_ref.1, bf16[192,720]{1,0:T(8,128)(2,1)} %dy_ref.1, f32[8,192]{1,0:T(8,128)} %pad_maximum_fusion.meta_ref, bf16[720,2880]{1,0:T(8,128)(2,1)} %bitcast.8, bf16[720,2880]{1,0:T(8,128)(2,1)} %bitcast.9, ...), custom_call_target="tpu_custom_call" | custom-call | tf_op jit(solution)/shard_map/pallas_call | solution.py:509
  152.5 1.3 slice_bitcast_fusion
  153.8 0.0 copy-start
  153.8 11.7 %slice_convert_fusion = (f32[1,720,2880]{2,1,0:T(8,128)}, f32[1,720,2880]{2,1,0:T(8,128)}, f32[1,720,2880]{2,1,0:T(8,128)}) fusion(bf16[3,720,2880]{2,1,0:T(8,128)(2,1)} %get-tuple-element.10), kind=kLoop, calls=%fused_computation | loop fusion | flops 6220800 | bytes 37324800 | tf_op jit(solution)/shard_map/convert_element_type | solution.py:553
  165.5 0.0 copy-done
  165.5 0.7 copy.13
Async XLA Ops:
  153.8 11.7 %copy-start = (bf16[192,720]{1,0:T(8,128)(2,1)S(1)}, bf16[192,720]{1,0:T(8,128)(2,1)}, u32[]{:S(2)}) copy-start(bf16[192,720]{1,0:T(8,128)(2,1)} %get-tuple-element.19) | copy-start | bytes 829444

commit v2 on v1

--- a/solution.py
+++ b/solution.py
@@ -161,9 +161,9 @@
 
 
 def fused_kernel(
-    n_expert, x_ref, dy_ref, meta_ref, wg_hbm, wu_hbm, wd_hbm,
+    n_expert, x_ref, dy_ref, ids_ref, rw_ref, wg_hbm, wu_hbm, wd_hbm,
     w, grad_out, route_out,
-    g, gm, d, tok, got_a, got_bx, got_by, got_c, got_d,
+    g, meta_ref, gm, d, tok, got_a, got_bx, got_by, got_c, got_d,
     route, route_x, route_s, route_y, route_t, route_z,
     own_sem, zs, zr, xsem, xr, ysem, yr, ds, dr, ss, sr, ms, mr, w_sem,
     sa, ra, sbx, rbx, sby, rby, sc, rc, sd, rd, sroute, rroute, srx, rrx,
@@ -181,6 +181,9 @@
     ]
     for copy in load:
         copy.start()
+    top = ids_ref.shape[0]
+    meta_ref[:top] = ids_ref[...].astype(F32)
+    meta_ref[top:] = rw_ref[...]
     greet(n_expert, e, h, across_x, across_y)
     full = (x_ref, dy_ref)
 
@@ -196,11 +199,18 @@
     def meta_to(i):
         return send(meta_ref, gm.at[e], ms.at[i], mr.at[i], ((e + n_expert - i) % n_expert, h))
 
+    def apart(j):
+        return j + (j // 2) * (5 - 2 * j)
+
+    def plane_of(j):
+        return flip(z, apart(j))
+
     def column(j):
-        return flip(z, j) * 2 + core
-
-    def z_send(t, i):
-        return send(full[t], block(t, e, h), zs.at[t, i], zr.at[t, i], (column(i), h))
+        return plane_of(j) * 2 + core
+
+    def z_send(t, j):
+        i = apart(j)
+        return send(full[t], block(t, e, h), zs.at[t, i], zr.at[t, i], (column(j), h))
 
     def first_sends(t, j, src):
         slot = block(t, column(j), h)
@@ -233,7 +243,8 @@
             copy.wait_send()
 
     def first(t, j):
-        arrived(block(t, column(j), h), zs.at[t, j], zr.at[t, j], across_x)
+        i = apart(j)
+        arrived(block(t, column(j), h), zs.at[t, i], zr.at[t, i], across_x)
         start(first_sends(t, j, None))
 
     def second(t, j):
@@ -248,25 +259,23 @@
         start(third_sends(t, j))
 
     def from_sibling(t, j):
-        b = flip(z, j) * 2 + (1 - core)
+        b = plane_of(j) * 2 + (1 - core)
         for k, part in enumerate((h, hx, hy, hd)):
             arrived(block(t, b, part), ss.at[t, j, k], sr.at[t, j, k], sibling)
 
     start(first_sends(0, 0, x_ref))
     start([meta_to(i) for i in range(1, n_expert)])
-    for t in range(2):
-        z_send(t, 1).start()
+    z_send(0, 1).start()
     start(first_sends(1, 0, dy_ref))
+    z_send(1, 1).start()
+    for j in range(2, nz):
+        for t in range(2):
+            z_send(t, j).start()
     start(own)
     second(0, 0)
     first(0, 1)
-    z_send(0, 2).start()
     second(1, 0)
     first(1, 1)
-    z_send(1, 2).start()
-    for i in range(3, nz):
-        for t in range(2):
-            z_send(t, i).start()
     third(0, 0)
     for copy in load + own:
         copy.wait()
@@ -279,16 +288,16 @@
     def add(a, b):
         return (a.astype(F32) + b.astype(F32)).astype(BF16)
 
-    def a_send(j):
-        return send(tok.at[1 - core], got_a.at[j], sa.at[j], ra.at[j], sibling)
+    def a_send(j, s):
+        return send(tok.at[1 - core, s], got_a.at[j, s], sa.at[j, s], ra.at[j, s], sibling)
 
     def b_sends(j):
         return [
             send(got_a.at[j, k * 2 + (1 - x), low], got_bx.at[j, k], sbx.at[j, k], rbx.at[j, k], across_x)
-            for k in range(2)
+            for k in (1 - y, y)
         ] + [
             send(got_a.at[j, (1 - y) * 2 + k, high], got_by.at[j, k], sby.at[j, k], rby.at[j, k], across_y)
-            for k in range(2)
+            for k in (1 - x, x)
         ]
 
     def c_sends(j):
@@ -298,26 +307,32 @@
         ]
 
     def d_send(j):
-        return send(got_c.at[j], got_d.at[j], sd.at[j], rd.at[j], (column(j), h))
+        i = apart(j)
+        return send(got_c.at[j], got_d.at[i], sd.at[i], rd.at[i], (column(j), h))
 
     def fold(j):
-        a_send(j).wait()
         for s in range(shares):
+            a_send(j, s).wait()
             got_a[j, s] = add(tok[core, s], got_a[j, s])
 
     def stage_b(j):
         start(b_sends(j))
 
     def stage_c(j):
-        copies = b_sends(j)
-        for k in range(2):
-            copies[k].wait_recv()
-            got_bx[j, k] = add(got_a[j, k * 2 + x, low], got_bx[j, k])
-            copies[2 + k].wait_recv()
-            got_by[j, k] = add(got_a[j, y * 2 + k, high], got_by[j, k])
-        start(c_sends(j))
+        near_x, near_y = b_sends(j)[0::2]
+        onward = c_sends(j)
+        near_x.wait_recv()
+        got_bx[j, 1 - y] = add(got_a[j, (1 - y) * 2 + x, low], got_bx[j, 1 - y])
+        onward[0].start()
+        near_y.wait_recv()
+        got_by[j, 1 - x] = add(got_a[j, y * 2 + (1 - x), high], got_by[j, 1 - x])
+        onward[1].start()
 
     def stage_d(j):
+        for copy in b_sends(j)[1::2]:
+            copy.wait_recv()
+        got_bx[j, y] = add(got_a[j, h, low], got_bx[j, y])
+        got_by[j, x] = add(got_a[j, h, high], got_by[j, x])
         for copy in c_sends(j):
             copy.wait_recv()
         got_c[j, low] = add(got_bx[j, y], got_c[j, low])
@@ -348,18 +363,13 @@
 
     def step(j, carry):
         more, further, final = j + 1 < nz, j + 2 < nz, j == last
-        plane = flip(z, j)
+        plane = plane_of(j)
         rows = pl.ds(pl.multiple_of(plane * (2 * count), 64), 2 * count)
         from_sibling(0, j)
 
         @pl.when(more)
         def _():
             second(0, j + 1)
-
-        @pl.when(final)
-        def _():
-            for i in range(1, last - 1):
-                stage_b(i)
 
         gate = project(0, rows, 0)
         up = project(0, rows, 1)
@@ -396,7 +406,6 @@
         d[1, rows] = (grad_hidden * act).astype(BF16)
         for c in range(2):
             per_token = jnp.sum(eye * parted[c * count : (c + 1) * count], axis=0, keepdims=True)
-            top = hits[c].shape[0]
             route[plane * 2 + c, :top] = hits[c] * per_token
             route[plane * 2 + c, top:] = jnp.zeros_like(hits[c])
 
@@ -408,6 +417,10 @@
         def _():
             first(1, j + 2)
 
+        @pl.when(j == last - 1)
+        def _():
+            stage_b(1)
+
         @pl.when(more)
         def _():
             third(0, j + 1)
@@ -415,8 +428,7 @@
         @pl.when(final)
         def _():
             rx.start()
-            for i in range(1, last - 1):
-                stage_c(i)
+            stage_c(1)
 
         for s in range(shares):
             row_grad = (
@@ -425,7 +437,14 @@
             ).astype(BF16)
             for c in range(2):
                 tok[c, s] = row_grad[c * count : (c + 1) * count]
-        a_send(j).start()
+            if s == 1:
+
+                @pl.when(final)
+                def _():
+                    stage_c(last - 1)
+
+        for s in range(shares):
+            a_send(j, s).start()
         return carry
 
     lax.fori_loop(0, nz, step, 0)
@@ -440,22 +459,27 @@
         route_t[...] = route_s[...] + route_y[...]
         start(routes)
 
-    def tail_one():
-        route_on()
-        for i in range(1, last - 1):
-            stage_d(i)
-        stage_c(last - 1)
+    def last_rows():
         fold(last)
         stage_b(last)
+        route_on()
+
+    def one_plane():
+        stage_d(1)
         stage_b(0)
 
+    def two_planes():
+        stage_d(last - 1)
+        route_out_to_owners()
+
     events = {
-        (0, 0): tail_one,
-        (0, 2): route_out_to_owners,
-        (0, 3): lambda: stage_d(last - 1),
-        (1, 1): lambda: stage_c(last),
-        (1, 3): lambda: stage_d(last),
-        (2, 1): lambda: stage_c(0),
+        (0, 0): last_rows,
+        (0, 1): one_plane,
+        (0, 2): two_planes,
+        (0, 3): lambda: stage_c(last),
+        (1, 1): lambda: stage_d(last),
+        (1, 2): lambda: stage_c(0),
+        (2, 0): lambda: stage_d(0),
     }
 
     def outer(m, carry):
@@ -469,16 +493,15 @@
         return carry
 
     lax.fori_loop(0, 3, outer, 0)
-    stage_d(0)
     total = route_t[e]
     for i in range(1, n_expert):
         routes[i - 1].wait_recv()
         total = total + route_z[i]
-    route_out[...] = total
+    route_out[...] = total[:top]
     total = got_c[0].astype(F32)
     for j in range(1, nz):
         d_send(j).wait_recv()
-        total = total + got_d[j].astype(F32)
+        total = total + got_d[apart(j)].astype(F32)
     grad_out[...] = total.astype(BF16)
     sent([rx, ry] + routes + [d_send(j) for j in range(1, nz)])
     for j in range(nz):
@@ -493,8 +516,10 @@
             sent(second_sends(t, j, 0) + second_sends(t, j, 1) + third_sends(t, j))
 
 
-def gather_and_expert(x, dy, meta, w_gate, w_up, w_down, n_expert):
+def gather_and_expert(x, dy, ids, route_weight, w_gate, w_up, w_down, n_expert):
     nz = n_expert // 2
+    top = ids.shape[0]
+    meta = (2 * top, ids.shape[1])
     count, width = x.shape
     hidden, depth = w_gate.shape
     total = n_expert * count
@@ -509,15 +534,16 @@
     return pl.pallas_call(
         functools.partial(fused_kernel, n_expert),
         out_shape=(
-            jax.ShapeDtypeStruct((3, hidden, depth), BF16),
+            room(3, hidden, depth),
             jax.ShapeDtypeStruct((count, width), BF16),
-            jax.ShapeDtypeStruct(meta.shape, F32),
+            jax.ShapeDtypeStruct(ids.shape, F32),
         ),
-        in_specs=[vmem] * 3 + [hbm] * 3,
+        in_specs=[vmem] * 4 + [hbm] * 3,
         out_specs=[vmem] * 3,
         scratch_shapes=[
             room(2, 4, total, width),
-            pltpu.VMEM((n_expert,) + meta.shape, F32),
+            pltpu.VMEM(meta, F32),
+            pltpu.VMEM((n_expert,) + meta, F32),
             room(3, total, hidden),
             room(2, 4, count, width),
             room(nz, 4, count, width),
@@ -526,32 +552,30 @@
             room(nz, count, width),
             room(nz, count, width),
         ]
-        + [pltpu.VMEM((n_expert,) + meta.shape, F32)] * 6
+        + [pltpu.VMEM((n_expert,) + meta, F32)] * 6
         + [dma((3,))]
         + [dma((2, nz))] * 6
         + [dma((2, nz, 2))] * 2
         + [dma((2, nz, 4))] * 2
         + [dma((n_expert,))] * 2
         + [dma((3,))]
-        + [dma((nz,))] * 2
+        + [dma((nz, 4))] * 2
         + [dma((nz, 2))] * 6
         + [dma((nz,))] * 2
         + [dma((n_expert,))] * 2
         + [dma((2,))] * 2,
         compiler_params=pltpu.CompilerParams(
-            collective_id=0, has_side_effects=True, vmem_limit_bytes=63 * 1024 * 1024
+            collective_id=0, has_side_effects=True, vmem_limit_bytes=50 * 1024 * 1024
         ),
-    )(x, dy, meta, w_gate, w_up, w_down)
+    )(x, dy, ids, route_weight, w_gate, w_up, w_down)
 
 
 def paired_device(inputs, out_grad, expert_ids, route_weight, w_gate, w_up, w_down):
-    top = expert_ids.shape[1]
-    meta = jnp.concatenate([expert_ids.astype(F32).T, route_weight.T], axis=0)
     grads, grad_input, grad_route = gather_and_expert(
-        inputs, out_grad, meta, w_gate[0], w_up[0], w_down[0], lax.axis_size("expert")
+        inputs, out_grad, expert_ids.T, route_weight.T, w_gate[0], w_up[0], w_down[0], lax.axis_size("expert")
     )
     wide = [grads[i].astype(F32)[None] for i in range(3)]
-    return (grad_input, grad_route[:top].T, *wide)
+    return (grad_input, grad_route.T, *wide)
 
 
 def solution(mesh):

time: 167 us -> 155 us (0.928)
  Pallas kernels: 150 us -> 144 us
  other arithmetic: 13.7 us -> 8.83 us
    pallas_call x1, Pallas kernels: 150 us -> 144 us  [gather_and_expert(): pl.pallas_call(functools.partial(fused_kernel, n_expert), out_shape=(room...]
    convert_element_type x1, other arithmetic: 11.7 us -> 8.83 us  [paired_device(): wide = [grads[i].astype(F32)[None] for i in range(3)]]
where the time goes in v2:
time: 155 us
  Pallas kernels  144 us (93%)
  other arithmetic  8.83 us (6%)
    pallas_call x1, Pallas kernels, gather_and_expert(): pl.pallas_call(functools.partial(fused_kernel, n_expert), out_shape=(room...  144 us
    convert_element_type x1, other arithmetic, paired_device(): wide = [grads[i].astype(F32)[None] for i in range(3)]  8.83 us

profile of v2, /device:TPU:0, one launch (start us, length us, event | category | flops | bytes accessed | tf_op | source)
XLA Modules:
  0.0 155.0 jit_solution(9257069633487911604)
XLA Ops:
  0.6 144.2 %shard_map.110 = (bf16[3,720,2880]{2,1,0:T(8,128)(2,1)S(1)}, bf16[192,720]{1,0:T(8,128)(2,1)}, f32[4,192]{1,0:T(4,128)}) custom-call(bf16[192,720]{1,0:T(8,128)(2,1)} %x_ref.1, bf16[192,720]{1,0:T(8,128)(2,1)} %dy_ref.1, s32[4,192]{1,0:T(4,128)} %bitcast.9, f32[4,192]{1,0:T(4,128)} %bitcast.10, bf16[720,2880]{1,0:T(8,128)(2,1)} %bitcast.6, ...), custom_call_target="tpu_custom_call" | custom-call | tf_op jit(solution)/shard_map/pallas_call | solution.py:534
  144.8 0.0 copy-start
  144.8 0.0 copy-start.1
  144.8 8.8 %slice_convert_fusion = (f32[1,720,2880]{2,1,0:T(8,128)}, f32[1,720,2880]{2,1,0:T(8,128)}, f32[1,720,2880]{2,1,0:T(8,128)}) fusion(bf16[3,720,2880]{2,1,0:T(8,128)(2,1)S(1)} %get-tuple-element.10), kind=kLoop, calls=%fused_computation | loop fusion | flops 6220800 | bytes 37324800 | tf_op jit(solution)/shard_map/convert_element_type | solution.py:577
  153.7 0.0 copy-done
  153.7 0.7 copy.14
  154.4 0.0 copy-done.1
  154.4 0.6 copy.15
Async XLA Ops:
  144.8 8.8 %copy-start = (bf16[192,720]{1,0:T(8,128)(2,1)S(1)}, bf16[192,720]{1,0:T(8,128)(2,1)}, u32[]{:S(2)}) copy-start(bf16[192,720]{1,0:T(8,128)(2,1)} %get-tuple-element.19) | copy-start | bytes 829444
  144.8 9.6 %copy-start.1 = (f32[4,192]{1,0:T(4,128)S(1)}, f32[4,192]{1,0:T(4,128)}, u32[]{:S(2)}) copy-start(f32[4,192]{1,0:T(4,128)} %get-tuple-element.9) | copy-start | bytes 9220

commit v3 on v2

--- a/solution.py
+++ b/solution.py
@@ -437,12 +437,6 @@
             ).astype(BF16)
             for c in range(2):
                 tok[c, s] = row_grad[c * count : (c + 1) * count]
-            if s == 1:
-
-                @pl.when(final)
-                def _():
-                    stage_c(last - 1)
-
         for s in range(shares):
             a_send(j, s).start()
         return carry
@@ -462,10 +456,11 @@
     def last_rows():
         fold(last)
         stage_b(last)
+        stage_d(1)
         route_on()
 
-    def one_plane():
-        stage_d(1)
+    def last_on():
+        stage_c(last)
         stage_b(0)
 
     def two_planes():
@@ -474,12 +469,11 @@
 
     events = {
         (0, 0): last_rows,
-        (0, 1): one_plane,
-        (0, 2): two_planes,
-        (0, 3): lambda: stage_c(last),
+        (0, 1): two_planes,
+        (0, 3): last_on,
         (1, 1): lambda: stage_d(last),
-        (1, 2): lambda: stage_c(0),
-        (2, 0): lambda: stage_d(0),
+        (1, 3): lambda: stage_c(0),
+        (2, 1): lambda: stage_d(0),
     }
 
     def outer(m, carry):
@@ -492,6 +486,7 @@
                     pl.when(m == at_m)(event)
         return carry
 
+    stage_c(last - 1)
     lax.fori_loop(0, 3, outer, 0)
     total = route_t[e]
     for i in range(1, n_expert):

time: 155 us -> 153 us (0.987)
  Pallas kernels: 144 us -> 142 us
    pallas_call x1, Pallas kernels: 144 us -> 142 us  [gather_and_expert(): pl.pallas_call(functools.partial(fused_kernel, n_expert), out_shape=(room...]
where the time goes in v3:
time: 153 us; the launch traced here: 152 us
  Pallas kernels  142 us (93%)
  other arithmetic  8.83 us (6%)
    pallas_call x1, Pallas kernels, gather_and_expert(): pl.pallas_call(functools.partial(fused_kernel, n_expert), out_shape=(room...  142 us
    convert_element_type x1, other arithmetic, paired_device(): wide = [grads[i].astype(F32)[None] for i in range(3)]  8.83 us

profile of v3, /device:TPU:0, one launch (start us, length us, event | category | flops | bytes accessed | tf_op | source)
XLA Modules:
  0.0 152.4 jit_solution(15603872643825764273)
XLA Ops:
  0.6 141.6 %shard_map.110 = (bf16[3,720,2880]{2,1,0:T(8,128)(2,1)S(1)}, bf16[192,720]{1,0:T(8,128)(2,1)}, f32[4,192]{1,0:T(4,128)}) custom-call(bf16[192,720]{1,0:T(8,128)(2,1)} %x_ref.1, bf16[192,720]{1,0:T(8,128)(2,1)} %dy_ref.1, s32[4,192]{1,0:T(4,128)} %bitcast.9, f32[4,192]{1,0:T(4,128)} %bitcast.10, bf16[720,2880]{1,0:T(8,128)(2,1)} %bitcast.6, ...), custom_call_target="tpu_custom_call" | custom-call | tf_op jit(solution)/shard_map/pallas_call | solution.py:529
  142.3 0.0 copy-start
  142.3 0.0 copy-start.1
  142.3 8.8 %slice_convert_fusion = (f32[1,720,2880]{2,1,0:T(8,128)}, f32[1,720,2880]{2,1,0:T(8,128)}, f32[1,720,2880]{2,1,0:T(8,128)}) fusion(bf16[3,720,2880]{2,1,0:T(8,128)(2,1)S(1)} %get-tuple-element.10), kind=kLoop, calls=%fused_computation | loop fusion | flops 6220800 | bytes 37324800 | tf_op jit(solution)/shard_map/convert_element_type | solution.py:572
  151.1 0.0 copy-done
  151.1 0.7 copy.14
  151.8 0.0 copy-done.1
  151.8 0.6 copy.15
Async XLA Ops:
  142.3 8.8 %copy-start = (bf16[192,720]{1,0:T(8,128)(2,1)S(1)}, bf16[192,720]{1,0:T(8,128)(2,1)}, u32[]{:S(2)}) copy-start(bf16[192,720]{1,0:T(8,128)(2,1)} %get-tuple-element.19) | copy-start | bytes 829444
  142.3 9.6 %copy-start.1 = (f32[4,192]{1,0:T(4,128)S(1)}, f32[4,192]{1,0:T(4,128)}, u32[]{:S(2)}) copy-start(f32[4,192]{1,0:T(4,128)} %get-tuple-element.9) | copy-start | bytes 9220
